TPU v7x, 16 devices: a 4x2x1 block of a 4x4x8 slice. The times are simulated.
16 devices in a mesh: rep: 2 (over y, z), dp: 8 (over x, core).
Axes of the slice: x: 4, y: 2, z: 1, core: 2. Of those that a mesh axis runs over, the one named last changes fastest.
The devices are a block of a 4x4x8 slice.
Arguments:
- g_w_gate: bfloat16 [16, 2, 1536, 4096], P(('rep', 'dp')), parts along dimension 0
- g_w_up: bfloat16 [16, 2, 1536, 4096], P(('rep', 'dp')), parts along dimension 0
- g_w_down: bfloat16 [16, 2, 4096, 1536], P(('rep', 'dp')), parts along dimension 0
- w_gate: bfloat16 [2, 1536, 4096], replicated
- w_up: bfloat16 [2, 1536, 4096], replicated
- w_down: bfloat16 [2, 4096, 1536], replicated
- m_w_gate: float32 [2, 1536, 4096], P(None, 'dp')
- m_w_up: float32 [2, 1536, 4096], P(None, 'dp')
- m_w_down: float32 [2, 4096, 1536], P(None, 'dp')
- v_w_gate: float32 [2, 1536, 4096], P(None, 'dp')
- v_w_up: float32 [2, 1536, 4096], P(None, 'dp')
- v_w_down: float32 [2, 4096, 1536], P(None, 'dp')
Outputs:
- output 1: bfloat16 [4, 1536, 4096], P('rep'), parts along dimension 0
- output 2: bfloat16 [4, 1536, 4096], P('rep'), parts along dimension 0
- output 3: bfloat16 [4, 4096, 1536], P('rep'), parts along dimension 0
- output 4: float32 [4, 1536, 4096], P('rep', 'dp'), parts along dimension 0
- output 5: float32 [4, 1536, 4096], P('rep', 'dp'), parts along dimension 0
- output 6: float32 [4, 4096, 1536], P('rep', 'dp'), parts along dimension 0
- output 7: float32 [4, 1536, 4096], P('rep', 'dp'), parts along dimension 0
- output 8: float32 [4, 1536, 4096], P('rep', 'dp'), parts along dimension 0
- output 9: float32 [4, 4096, 1536], P('rep', 'dp'), parts along dimension 0
There are 2 independent parts. A program takes and returns all parts, laid end to end along the dimension named above; an argument that names none is the same for every part.
All inputs are finite; a program needn't handle non-finite values.
Results may differ from a plain program's by a relative error of at most 0.022.
Values are sent between devices in bfloat16 or wider.
A program may use at most 768 MiB of HBM per device.

v0:
```python
import jax
import jax.numpy as jnp
from jax import lax
from jax.sharding import PartitionSpec as P


def adamw(w, m, v, g):
    m = 0.9 * m + 0.1 * g
    v = 0.95 * v + 0.05 * g * g
    step = m * lax.rsqrt(v + 1e-8) + 0.1 * w
    return (w - 0.02 * step).astype(jnp.bfloat16), m, v


def solution(mesh):
    def step(*arrays):
        terms, weights, m, v = (arrays[i : i + 3] for i in (0, 3, 6, 9))
        gradients = [lax.psum_scatter(t[0], "dp", scatter_dimension=1, tiled=True).astype(jnp.float32) for t in terms]
        me = lax.axis_index("dp")
        own = [lax.dynamic_slice_in_dim(w, me * one.shape[1], one.shape[1], 1).astype(jnp.float32) for w, one in zip(weights, m, strict=True)]
        new = [adamw(w, m, v, g) for w, m, v, g in zip(own, m, v, gradients, strict=True)]
        whole = [lax.all_gather(one[0], "dp", axis=1, tiled=True) for one in new]
        return (*whole, *(one[1] for one in new), *(one[2] for one in new))

    all_of, cut = P(None, None, None), P(None, "dp", None)
    return jax.shard_map(
        step,
        mesh=mesh,
        in_specs=(P(("rep", "dp"), None, None, None),) * 3 + (all_of,) * 3 + (cut,) * 6,
        out_specs=(P("rep", None, None),) * 3 + (P("rep", "dp", None),) * 6,
        check_vma=False,
    )
```

profile of v0, /device:TPU:113, one launch (start us, length us, event | category | flops | bytes accessed | tf_op | source)
XLA Modules:
  0.0 819.3 jit_solution(11649683465932915007)
XLA Ops:
  7.2 0.1 reduce-scatter.8.cloned.1.call-start
  7.3 0.7 reduce-scatter.8.cloned.1.call-update
  8.0 0.1 reduce-scatter.6.cloned.1.call-start
  8.1 0.7 reduce-scatter.6.cloned.1.call-update
  8.8 0.1 reduce-scatter.4.cloned.1.call-start
  8.9 0.7 reduce-scatter.4.cloned.1.call-update
  9.6 0.1 all-gather.8.cloned.1.call-start
  9.7 130.5 %reduce-scatter.8.cloned.1.call-done = bf16[2,512,1536]{2,1,0:T(8,128)(2,1)} async-done(((bf16[2,4096,1536]{2,1,0:T(8,128)(2,1)}), bf16[2,512,1536]{2,1,0:T(8,128)(2,1)}) %reduce-scatter.8.cloned.1.call-update) | async-done | bytes 3145744 | tf_op jit(solution)/shard_map/reduce_scatter | solution.py:17
  140.2 12.7 %fusion.10 = (bf16[2,512,1536]{2,1,0:T(8,128)(2,1)}, f32[2,512,1536]{2,1,0:T(8,128)}, f32[2,512,1536]{2,1,0:T(8,128)}) fusion(bf16[2,4096,1536]{2,1,0:T(8,128)(2,1)} %param.17, s32[]{:T(128)S(6)} %select_n.8, bf16[2,512,1536]{2,1,0:T(8,128)(2,1)} %reduce-scatter.8.cloned.1.call-done, f32[2,512,1536]{2,1,0:T(8,128)} %param.23, f32[2,512,1536]{2,1,0:T(8,128)} %param.20), kind=kLoop, calls=%fused_computation.22 | loop fusion | flops 25165824 | bytes 34603012 | tf_op jit(solution)/shard_map/convert_element_type | solution.py:11
  152.9 0.1 all-gather.8.cloned.1.call-update
  153.0 0.1 all-gather.6.cloned.1.call-start
  153.0 116.6 %reduce-scatter.6.cloned.1.call-done = bf16[2,192,4096]{2,1,0:T(8,128)(2,1)} async-done(((bf16[2,1536,4096]{2,1,0:T(8,128)(2,1)}), bf16[2,192,4096]{2,1,0:T(8,128)(2,1)}) %reduce-scatter.6.cloned.1.call-update) | async-done | bytes 3145744 | tf_op jit(solution)/shard_map/reduce_scatter | solution.py:17
  269.6 12.9 %fusion.6 = (bf16[2,192,4096]{2,1,0:T(8,128)(2,1)}, f32[2,192,4096]{2,1,0:T(8,128)}, f32[2,192,4096]{2,1,0:T(8,128)}) fusion(bf16[2,1536,4096]{2,1,0:T(8,128)(2,1)} %param.16, s32[]{:T(128)S(6)} %select_n.7, bf16[2,192,4096]{2,1,0:T(8,128)(2,1)} %reduce-scatter.6.cloned.1.call-done, f32[2,192,4096]{2,1,0:T(8,128)} %param.22, f32[2,192,4096]{2,1,0:T(8,128)} %param.19), kind=kLoop, calls=%fused_computation.18 | loop fusion | flops 25165824 | bytes 34603012 | tf_op jit(solution)/shard_map/convert_element_type | solution.py:11
  282.4 0.1 all-gather.6.cloned.1.call-update
  282.5 0.1 all-gather.4.cloned.1.call-start
  282.6 116.4 %reduce-scatter.4.cloned.1.call-done = bf16[2,192,4096]{2,1,0:T(8,128)(2,1)} async-done(((bf16[2,1536,4096]{2,1,0:T(8,128)(2,1)}), bf16[2,192,4096]{2,1,0:T(8,128)(2,1)}) %reduce-scatter.4.cloned.1.call-update) | async-done | bytes 3145744 | tf_op jit(solution)/shard_map/reduce_scatter | solution.py:17
  399.0 12.9 %fusion.2 = (bf16[2,192,4096]{2,1,0:T(8,128)(2,1)}, f32[2,192,4096]{2,1,0:T(8,128)}, f32[2,192,4096]{2,1,0:T(8,128)}) fusion(bf16[2,1536,4096]{2,1,0:T(8,128)(2,1)} %param.15, s32[]{:T(128)S(6)} %select_n.7, bf16[2,192,4096]{2,1,0:T(8,128)(2,1)} %reduce-scatter.4.cloned.1.call-done, f32[2,192,4096]{2,1,0:T(8,128)} %param.21, f32[2,192,4096]{2,1,0:T(8,128)} %param.18), kind=kLoop, calls=%fused_computation.14 | loop fusion | flops 25165824 | bytes 34603012 | tf_op jit(solution)/shard_map/convert_element_type | solution.py:11
  411.8 0.1 all-gather.4.cloned.1.call-update
  411.9 106.4 %all-gather.8.cloned.1.call-done = bf16[2,4096,1536]{2,1,0:T(8,128)(2,1)} async-done(((bf16[2,512,1536]{2,1,0:T(8,128)(2,1)}), bf16[2,4096,1536]{2,1,0:T(8,128)(2,1)}) %all-gather.8.cloned.1.call-update) | async-done | bytes 25165840 | tf_op jit(solution)/shard_map/all_gather | solution.py:21
  518.3 119.6 %all-gather.6.cloned.1.call-done = bf16[2,1536,4096]{2,1,0:T(8,128)(2,1)} async-done(((bf16[2,192,4096]{2,1,0:T(8,128)(2,1)}), bf16[2,1536,4096]{2,1,0:T(8,128)(2,1)}) %all-gather.6.cloned.1.call-update) | async-done | bytes 25165840 | tf_op jit(solution)/shard_map/all_gather | solution.py:21
  637.9 119.6 %all-gather.4.cloned.1.call-done = bf16[2,1536,4096]{2,1,0:T(8,128)(2,1)} async-done(((bf16[2,192,4096]{2,1,0:T(8,128)(2,1)}), bf16[2,1536,4096]{2,1,0:T(8,128)(2,1)}) %all-gather.4.cloned.1.call-update) | async-done | bytes 25165840 | tf_op jit(solution)/shard_map/all_gather | solution.py:21
  757.6 0.0 slice-start
  757.6 0.0 slice-start.1
  757.6 0.0 slice-start.2
  757.6 23.0 %copy.24 = bf16[2,1536,4096]{2,1,0:T(8,128)(2,1)} copy(bf16[2,1536,4096]{2,1,0:T(8,128)(2,1)} %all-gather.4.cloned.1.call-done) | data formatting | bytes 50331648
  780.5 0.0 slice-start.3
  780.5 0.0 slice-start.4
  780.5 0.0 slice-start.5
  780.5 23.0 %copy.25 = bf16[2,1536,4096]{2,1,0:T(8,128)(2,1)} copy(bf16[2,1536,4096]{2,1,0:T(8,128)(2,1)} %all-gather.6.cloned.1.call-done) | data formatting | bytes 50331648
  803.5 0.0 slice-done
  803.5 0.0 slice-done.1
  803.5 0.0 slice-done.2
  803.5 0.0 slice-done.3
  803.5 0.0 slice-done.4
  803.5 0.0 slice-done.5
  803.5 8.9 %copy.26 = bf16[2,4096,1536]{2,1,0:T(8,128)(2,1)} copy(bf16[2,4096,1536]{2,1,0:T(8,128)(2,1)S(1)} %bitcast.7) | data formatting | bytes 50331648
  (1 shorter events, 0.0 us)
Async XLA Ops:
  7.2 133.0 %reduce-scatter.8.cloned.1.call-start = ((), (), s32[]{:S(2)}) async-start(), calls=%async_computation.7 | async-start | bytes 28311552 | tf_op jit(solution)/shard_map/reduce_scatter | solution.py:17
  8.0 261.6 %reduce-scatter.6.cloned.1.call-start = ((), (), s32[]{:S(2)}) async-start(), calls=%async_computation.5 | async-start | bytes 28311552 | tf_op jit(solution)/shard_map/reduce_scatter | solution.py:17
  8.8 390.2 %reduce-scatter.4.cloned.1.call-start = ((), (), s32[]{:S(2)}) async-start(), calls=%async_computation.3 | async-start | bytes 28311552 | tf_op jit(solution)/shard_map/reduce_scatter | solution.py:17
  9.6 508.7 %all-gather.8.cloned.1.call-start = ((), (), s32[]{:S(2)}) async-start(), calls=%async_computation.8 | async-start | bytes 28311552 | tf_op jit(solution)/shard_map/all_gather | solution.py:21
  153.0 485.0 %all-gather.6.cloned.1.call-start = ((), (), s32[]{:S(2)}) async-start(), calls=%async_computation.6 | async-start | bytes 28311552 | tf_op jit(solution)/shard_map/all_gather | solution.py:21
  282.5 475.1 %all-gather.4.cloned.1.call-start = ((), (), s32[]{:S(2)}) async-start(), calls=%async_computation.4 | async-start | bytes 28311552 | tf_op jit(solution)/shard_map/all_gather | solution.py:21
  757.6 45.9 %slice-start = ((s8[25165824]{0:T(1024)(128)(4,1)}), s8[4194304]{0:T(1024)(128)(4,1)S(1)}, s32[]{:S(2)}) async-start(s8[25165824]{0:T(1024)(128)(4,1)} %bitcast.6), calls=%async_computation.9 | async-start | bytes 8388608
  757.6 45.9 %slice-start.1 = ((s8[25165824]{0:T(1024)(128)(4,1)}), s8[4194304]{0:T(1024)(128)(4,1)S(1)}, s32[]{:S(2)}) async-start(s8[25165824]{0:T(1024)(128)(4,1)} %bitcast.6), calls=%async_computation.10 | async-start | bytes 8388608
  757.6 45.9 %slice-start.2 = ((s8[25165824]{0:T(1024)(128)(4,1)}), s8[4194304]{0:T(1024)(128)(4,1)S(1)}, s32[]{:S(2)}) async-start(s8[25165824]{0:T(1024)(128)(4,1)} %bitcast.6), calls=%async_computation.11 | async-start | bytes 8388608
  780.5 23.0 %slice-start.3 = ((s8[25165824]{0:T(1024)(128)(4,1)}), s8[4194304]{0:T(1024)(128)(4,1)S(1)}, s32[]{:S(2)}) async-start(s8[25165824]{0:T(1024)(128)(4,1)} %bitcast.6), calls=%async_computation.12 | async-start | bytes 8388608
  780.5 23.0 %slice-start.4 = ((s8[25165824]{0:T(1024)(128)(4,1)}), s8[4194304]{0:T(1024)(128)(4,1)S(1)}, s32[]{:S(2)}) async-start(s8[25165824]{0:T(1024)(128)(4,1)} %bitcast.6), calls=%async_computation.13 | async-start | bytes 8388608
  780.5 23.0 %slice-start.5 = ((s8[25165824]{0:T(1024)(128)(4,1)}), s8[4194304]{0:T(1024)(128)(4,1)S(1)}, s32[]{:S(2)}) async-start(s8[25165824]{0:T(1024)(128)(4,1)} %bitcast.6), calls=%async_computation.14 | async-start | bytes 8388608
Sparse Core Ops, SparseCore 0:
  10.4 129.7 reduce-scatter.7
  142.6 126.9 reduce-scatter.5
  271.9 126.9 reduce-scatter.3
  401.0 117.2 all-gather.7
  520.3 117.5 all-gather.5
  639.9 117.5 all-gather.3
where the time goes:
time: 820 us; the launch traced here: 819 us
  waiting for transfers between devices  711 us (87%)
  local copies, waits for them, and re-layouts  54.9 us (7%)
  other arithmetic  38.4 us (5%)
  between operations  14.2 us (2%)
    reduce_scatter x3, waiting for transfers between devices, step(): lax.psum_scatter(t[0], 'dp', scatter_dimension=1, tiled=True)  363 us
    all_gather x3, waiting for transfers between devices, step(): whole = [lax.all_gather(one[0], 'dp', axis=1, tiled=True) for one in new]  346 us
    unnamed x15, local copies, waits for them, and re-layouts  54.9 us
    convert_element_type x3, other arithmetic, adamw(): return ((w - 0.02 * step).astype(jnp.bfloat16), m, v)  38.4 us
  transfers between devices with their start and end apart: 6, of which 6 were waited for; matrix products, arithmetic and copies ran while one was open for 5% of the time, Pallas kernels for 0%

commit v1 on v0

v1 whole, which is shorter than its diff:
```python
import functools

import jax
import jax.numpy as jnp
from jax import lax
from jax.experimental import pallas as pl
from jax.experimental.pallas import tpu as pltpu
from jax.sharding import PartitionSpec as P

MESH = pl.DeviceIdType.MESH
F32, BF16 = jnp.float32, jnp.bfloat16
SPLIT = 2
GATHERED = 2
BATCH = 8
SLOTS = 5


def adamw(w, m, v, g):
    m = 0.9 * m + 0.1 * g
    v = 0.95 * v + 0.05 * g * g
    step = m * lax.rsqrt(v + 1e-8) + 0.1 * w
    return (w - 0.02 * step).astype(BF16), m, v


def tiles(x):
    *lead, rows, columns = x.shape
    x = x.reshape(*lead, rows // 8, 8, columns // 128, 128)
    return jnp.swapaxes(x, -3, -2).reshape(-1, 8, 128)


def untiles(x, shape):
    *lead, rows, columns = shape
    x = x.reshape(*lead, rows // 8, columns // 128, 8, 128)
    return jnp.swapaxes(x, -3, -2).reshape(shape)


def kernel(n, layers, *refs):
    weights = 3
    g, w, m, v = (refs[i * weights : (i + 1) * weights] for i in range(4))
    refs = refs[4 * weights :]
    gathered, block_out, sums = refs[:GATHERED], refs[GATHERED:weights], refs[weights : 2 * weights]
    (own, sib, s1, s2p, s2m, r1, r2p, r2m, mb, vb, wb, gb, new) = refs[2 * weights : 2 * weights + 13]
    (own_sem, sib_send, sib_recv, ring_send, ring_recv, mvw_sem, g_sem, ag_send, ag_recv, out_sem) = refs[2 * weights + 13 :]

    chips = n // 2
    me = lax.axis_index("dp")
    x, c = me // 2, me % 2
    right, left = (me + 2) % n, (me + n - 2) % n
    other = 2 * x + 1 - c
    opposite = (me + n // 2) % n
    block = g[0].shape[0] // layers // n
    layer = block * n
    size = block // SPLIT
    half = size // 2
    per_weight = layers * SPLIT
    chunks = weights * per_weight
    ag_chunks = GATHERED * per_weight

    barrier = pltpu.get_barrier_semaphore()
    for peer in (right, left, other):
        pl.semaphore_signal(barrier, inc=1, device_id={"dp": peer}, device_id_type=MESH)
    pl.semaphore_wait(barrier, 3)

    def place(k):
        unit, s = divmod(k, SPLIT)
        which, at = divmod(unit, layers)
        return which, at, s

    def at_whole(k, owner):
        _, at, s = place(k)
        return pl.ds(at * layer + owner * block + s * size, size)

    def at_block(k):
        _, at, s = place(k)
        return pl.ds(at * block + s * size, size)

    def first(ds):
        return pl.ds(ds.start, half)

    def last(ds):
        return pl.ds(ds.start + half, half)

    def remote(src, dst, send, recv, peer):
        return pltpu.make_async_remote_copy(
            src_ref=src, dst_ref=dst, send_sem=send, recv_sem=recv, device_id={"dp": peer}, device_id_type=MESH
        )

    def work(t):
        return [(k, js) for k, js in ((t + 1, (2,)), (t - 1, (1, 3)), (t - 3, (0,))) if 0 <= k < chunks]

    def own_copy(t, k, j):
        owner = (x + j) % chips * 2 + c
        return pltpu.make_async_copy(g[place(k)[0]].at[at_whole(k, owner)], own.at[t % 2, j], own_sem.at[t % 2, j])

    def sib_copy(t, k, j):
        owner = (x + j) % chips * 2 + 1 - c
        return remote(
            g[place(k)[0]].at[at_whole(k, owner)], sib.at[t % 4, j], sib_send.at[t % 2, j], sib_recv.at[t % 4, j], other
        )

    def mvw_copies(t, k):
        which = place(k)[0]
        return [
            pltpu.make_async_copy(m[which].at[at_block(k)], mb.at[t % 2], mvw_sem.at[t % 2, 0]),
            pltpu.make_async_copy(v[which].at[at_block(k)], vb.at[t % 2], mvw_sem.at[t % 2, 1]),
            pltpu.make_async_copy(w[which].at[at_whole(k, me)], wb.at[t % 2], mvw_sem.at[t % 2, 2]),
        ]

    def load(t):
        for k, js in work(t):
            for j in js:
                sib_copy(t, k, j).start()
                own_copy(t, k, j).start()
            if js == (0,):
                for copy in mvw_copies(t, k):
                    copy.start()

    def loaded(t, k, js):
        for j in js:
            own_copy(t, k, j).wait()
            sib_copy(t, k, j).wait()
        if js == (0,):
            for copy in mvw_copies(t, k):
                copy.wait()

    A, B = pl.ds(0, half), pl.ds(half, half)

    def ring1(t):
        return [
            remote(s1.at[t % 2, A], r1.at[t % SLOTS, A], ring_send.at[t % 2, 0], ring_recv.at[t % SLOTS, 0], right),
            remote(s1.at[t % 2, B], r1.at[t % SLOTS, B], ring_send.at[t % 2, 1], ring_recv.at[t % SLOTS, 1], left),
        ]

    def ring2(t):
        return [
            remote(s2p.at[t % 2], r2p.at[t % SLOTS], ring_send.at[t % 2, 2], ring_recv.at[t % SLOTS, 2], right),
            remote(s2m.at[t % 2], r2m.at[t % SLOTS], ring_send.at[t % 2, 3], ring_recv.at[t % SLOTS, 3], left),
        ]

    def rings(t):
        return (ring1(t) if 0 <= t < chunks else []) + (ring2(t) if 0 <= t - 2 < chunks else [])

    def each(count, body):
        def step(i, carry):
            body(pl.ds(pl.multiple_of(i * BATCH, BATCH), BATCH), i * BATCH)
            return carry

        lax.fori_loop(0, count // BATCH, step, 0)

    def pair(t, j, ds):
        return own[t % 2, j, ds].astype(F32) + sib[t % 4, j, ds].astype(F32)

    def stage1(t):
        def body(ds, _):
            s1[(t + 1) % 2, ds] = pair(t, 2, ds).astype(BF16)

        each(size, body)

    def stage2(t):
        def body(a, i):
            b = pl.ds(pl.multiple_of(half + i, BATCH), BATCH)
            s2p[(t + 1) % 2, a] = (pair(t, 1, a) + r1[(t - 1) % SLOTS, a].astype(F32)).astype(BF16)
            s2m[(t + 1) % 2, b] = (pair(t, 3, b) + r1[(t - 1) % SLOTS, b].astype(F32)).astype(BF16)
            s2p[(t + 1) % 2, b] = pair(t, 1, b).astype(BF16)
            s2m[(t + 1) % 2, a] = pair(t, 3, a).astype(BF16)

        each(half, body)

    def stage3(t, k):
        def body(ds, _):
            total = pair(t, 0, ds) + r2p[(t - 1) % SLOTS, ds].astype(F32) + r2m[(t - 1) % SLOTS, ds].astype(F32)
            total = total.astype(BF16)
            gb[t % 2, ds] = total
            new[k, ds] = adamw(wb[t % 2, ds].astype(F32), mb[t % 2, ds], vb[t % 2, ds], total.astype(F32))[0]

        each(size, body)

    def sum_out(t, k):
        return pltpu.make_async_copy(gb.at[t % 2], sums[place(k)[0]].at[at_block(k)], g_sem.at[t % 2])

    def block_copy(k):
        which = place(k)[0]
        return pltpu.make_async_copy(new.at[k], block_out[which - GATHERED].at[at_block(k)], out_sem.at[k])

    def local_copy(k):
        return pltpu.make_async_copy(new.at[k], gathered[place(k)[0]].at[at_whole(k, me)], out_sem.at[k])

    def spread(k, some=(0, 1, 2)):
        to = gathered[place(k)[0]].at[at_whole(k, me)]
        peers = right, left, other
        return [remote(new.at[k], to, ag_send.at[k, i], ag_recv.at[k, i], peers[i]) for i in some]

    def passed(k, i, owner, peer, part=None):
        ds = at_whole(k, owner)
        ref = gathered[place(k)[0]].at[part(ds) if part else ds]
        return remote(ref, ref, ag_send.at[k, i], ag_recv.at[k, i], peer)

    def forward(k):
        return [passed(k, 3, left, right, first), passed(k, 4, right, left, last)]

    def across(k):
        return [passed(k, 5, left, other), passed(k, 6, right, other)]

    def across_opposite(k):
        return [passed(k, 7, opposite, other)]

    ticks = range(-1, max(chunks + 3, ag_chunks + 8))
    load(-1)
    for t in ticks:
        for copy in rings(t - 1):
            copy.wait()
        k = t - 6
        if 0 <= k < ag_chunks:
            for copy in spread(k, (0, 1)):
                copy.wait_recv()
            for copy in forward(k) + across(k):
                copy.start()
        k = t - 8
        if 0 <= k < ag_chunks:
            for copy in forward(k):
                copy.wait_recv()
            for copy in across_opposite(k):
                copy.start()
        load(t + 1)
        for k, js in work(t):
            loaded(t, k, js)
            if js == (2,):
                stage1(t)
                for copy in ring1(t + 1):
                    copy.start()
            elif js == (1, 3):
                stage2(t)
                for copy in ring2(t + 1):
                    copy.start()
            else:
                if k >= 2:
                    sum_out(t - 2, k - 2).wait()
                stage3(t, k)
                sum_out(t, k).start()
                if k < ag_chunks:
                    for copy in spread(k):
                        copy.start()
                    local_copy(k).start()
                else:
                    block_copy(k).start()

    for k in range(max(chunks - 2, 0), chunks):
        sum_out(k + 3, k).wait()
    for k in range(ag_chunks, chunks):
        block_copy(k).wait()
    for k in range(ag_chunks):
        local_copy(k).wait()
        for copy in spread(k) + forward(k):
            copy.wait_send()
        spread(k, (2,))[0].wait_recv()
        for copy in across(k) + across_opposite(k):
            copy.wait()


def exchange(n, layers, terms, weights, m, v):
    everywhere = pl.BlockSpec(memory_space=pl.ANY)
    block = terms[0].shape[0] // layers // n
    size = block // SPLIT
    count = len(weights)
    chunks = count * layers * SPLIT
    ag_chunks = GATHERED * layers * SPLIT
    tile = (8, 128)
    buffer = lambda *lead, dtype=BF16: pltpu.VMEM((*lead, *tile), dtype)
    dma = pltpu.SemaphoreType.DMA
    out = pl.pallas_call(
        functools.partial(kernel, n, layers),
        out_shape=[jax.ShapeDtypeStruct(x.shape, BF16) for x in weights[:GATHERED]]
        + [jax.ShapeDtypeStruct(x.shape, BF16) for x in m[GATHERED:]]
        + [jax.ShapeDtypeStruct(x.shape, BF16) for x in m],
        in_specs=[everywhere] * (4 * count),
        out_specs=[everywhere] * (2 * count),
        scratch_shapes=[
            buffer(2, 4, size),
            buffer(4, 4, size),
            *[buffer(2, size)] * 3,
            *[buffer(SLOTS, size)] * 3,
            *[buffer(2, size, dtype=F32)] * 2,
            buffer(2, size),
            buffer(2, size),
            buffer(chunks, size),
            dma((2, 4)),
            dma((2, 4)),
            dma((4, 4)),
            dma((2, 4)),
            dma((SLOTS, 4)),
            dma((2, 3)),
            dma((2,)),
            dma((ag_chunks, 8)),
            dma((ag_chunks, 8)),
            dma((chunks,)),
        ],
        compiler_params=pltpu.CompilerParams(collective_id=0, has_side_effects=True, vmem_limit_bytes=62 * 2**20),
    )(*terms, *weights, *m, *v)
    return out[:GATHERED], out[GATHERED:count], out[count:]


def copy_kernel(x, *rest):
    rest[-1][...] = x[...]


def copied(x, whole=None, part=0, parts=1, into=None):
    steps = 8
    size = x.shape[0] // steps
    out = jax.ShapeDtypeStruct((x.shape[0] * parts, *x.shape[1:]), x.dtype)
    extra = [] if into is None else [into]
    return pl.pallas_call(
        copy_kernel,
        grid=(steps,),
        out_shape=out,
        in_specs=[pl.BlockSpec((size, 8, 128), lambda i: (i, 0, 0))] + [pl.BlockSpec(memory_space=pl.ANY)] * len(extra),
        out_specs=pl.BlockSpec((size, 8, 128), lambda i: (i + part * steps, 0, 0)),
        input_output_aliases={1: 0} if extra else {},
        cost_estimate=pl.CostEstimate(flops=0, bytes_accessed=2 * x.size * x.dtype.itemsize, transcendentals=0),
        compiler_params=pltpu.CompilerParams(vmem_limit_bytes=32 * 2**20),
    )(x, *extra)


def solution(mesh):
    n = mesh.shape["dp"]

    def step(*arrays):
        terms, weights, m, v = (arrays[i : i + 3] for i in (0, 3, 6, 9))
        layers = weights[0].shape[0]
        m_tiles, v_tiles = [tiles(a) for a in m], [tiles(a) for a in v]
        landed, blocks, sums = exchange(n, layers, [tiles(t[0]) for t in terms], [tiles(a) for a in weights], m_tiles, v_tiles)
        whole = []
        for one in blocks:
            parts = [lax.all_gather(p, "dp", axis=0, tiled=True) for p in jnp.split(one, layers)]
            result = None
            for i, part in enumerate(parts):
                result = copied(part, part=i, parts=layers, into=result)
            whole.append(result)
        whole = [copied(a) for a in landed] + whole
        new_m, new_v = [], []
        for mm, vv, s in zip(m_tiles, v_tiles, sums, strict=True):
            _, a, b = adamw(jnp.zeros((), F32), mm, vv, s.astype(F32))
            new_m.append(a)
            new_v.append(b)
        return (
            *(untiles(a, like.shape) for a, like in zip(whole, weights, strict=True)),
            *(untiles(a, like.shape) for a, like in zip(new_m, m, strict=True)),
            *(untiles(a, like.shape) for a, like in zip(new_v, v, strict=True)),
        )

    all_of, cut = P(None, None, None), P(None, "dp", None)
    return jax.shard_map(
        step,
        mesh=mesh,
        in_specs=(P(("rep", "dp"), None, None, None),) * 3 + (all_of,) * 3 + (cut,) * 6,
        out_specs=(P("rep", None, None),) * 3 + (P("rep", "dp", None),) * 6,
        check_vma=False,
    )
```

time: 820 us -> 676 us (0.82)
  waiting for transfers between devices: 711 us -> 55.4 us
  Pallas kernels: 0 us -> 569 us
  local copies, waits for them, and re-layouts: 54.9 us -> 12.9 us
  other arithmetic: 38.4 us -> 24.5 us
    pallas_call x0 -> x5, Pallas kernels: none -> 569 us  [the longest x1 518 us: exchange(): pl.pallas_call(functools.partial(kernel, n, layers), out_shape=[jax.Shape...]
    reduce_scatter x3 -> x0, waiting for transfers between devices: 363 us -> none  [step(): lax.psum_scatter(t[0], 'dp', scatter_dimension=1, tiled=True)]
    all_gather x3 -> x2, waiting for transfers between devices: 346 us -> 54.7 us  [step(): lax.all_gather(p, 'dp', axis=0, tiled=True)]
    unnamed x15 -> x16, local copies, waits for them, and re-layouts: 54.9 us -> 9.18 us
    convert_element_type x3 -> x0, other arithmetic: 38.4 us -> none  [adamw(): return ((w - 0.02 * step).astype(jnp.bfloat16), m, v)]
    add x0 -> x2, other arithmetic: none -> 24.5 us  [adamw(): v = 0.95 * v + 0.05 * g * g]
  transfers between devices with their start and end apart: 6 -> 2, of which waited for: 6 -> 1; matrix products, arithmetic and copies ran while one was open for 5% -> 4% of each run, Pallas kernels for 0% -> 7%
where the time goes in v1:
time: 676 us
  Pallas kernels  569 us (84%)
  waiting for transfers between devices  55.4 us (8%)
  other arithmetic  24.5 us (4%)
  between operations  14.2 us (2%)
  local copies, waits for them, and re-layouts  12.9 us (2%)
    pallas_call x1, Pallas kernels, exchange(): pl.pallas_call(functools.partial(kernel, n, layers), out_shape=[jax.Shape...  518 us
    all_gather x2, waiting for transfers between devices, step(): lax.all_gather(p, 'dp', axis=0, tiled=True)  54.7 us
    pallas_call x4, Pallas kernels, copied(): pl.pallas_call(copy_kernel, grid=(steps,), out_shape=out, in_specs=[pl.Bl...  50.8 us
    add x2, other arithmetic, adamw(): v = 0.95 * v + 0.05 * g * g  24.5 us
  transfers between devices with their start and end apart: 2, of which 1 were waited for; matrix products, arithmetic and copies ran while one was open for 4% of the time, Pallas kernels for 7%

profile of v1, /device:TPU:113, one launch (start us, length us, event | category | flops | bytes accessed | tf_op | source)
XLA Modules:
  0.0 676.1 jit_solution(11916042385310830168)
XLA Ops:
  7.2 0.1 all-gather.5.cloned.1.call-start
  7.3 518.1 %shard_map.187 = (bf16[12288,8,128]{2,1,0:T(8,128)(2,1)}, bf16[12288,8,128]{2,1,0:T(8,128)(2,1)}, bf16[1536,8,128]{2,1,0:T(8,128)(2,1)}, bf16[1536,8,128]{2,1,0:...) custom-call(bf16[12288,8,128]{2,1,0:T(8,128)(2,1)} %bitcast.124, ...), custom_call_target="tpu_custom_call" | custom-call | tf_op jit(solution)/shard_map/pallas_call | solution.py:270
  525.3 3.8 fusion.6
  529.1 0.1 all-gather.5.cloned.1.call-update
  529.1 0.1 all-gather.3.cloned.1.call-start
  529.2 0.7 all-gather.3.cloned.1.call-update
  530.0 0.0 slice-start
  530.0 0.0 slice-start.2
  530.0 20.1 %shard_map.188 = bf16[12288,8,128]{2,1,0:T(8,128)(2,1)} custom-call(bf16[12288,8,128]{2,1,0:T(8,128)(2,1)} %get-tuple-element.15.x), custom_call_target="tpu_custom_call" | custom-call | bytes 50331648 | tf_op jit(solution)/shard_map/pallas_call | solution.py:311
  550.0 0.0 slice-start.1
  550.0 0.0 slice-start.3
  550.0 0.0 copy-start.3
  550.0 19.8 %shard_map.189 = bf16[12288,8,128]{2,1,0:T(8,128)(2,1)} custom-call(bf16[12288,8,128]{2,1,0:T(8,128)(2,1)} %get-tuple-element.16.x), custom_call_target="tpu_custom_call" | custom-call | bytes 50331648 | tf_op jit(solution)/shard_map/pallas_call | solution.py:311
  569.8 0.0 slice-done
  569.8 0.0 slice-done.2
  569.8 0.0 slice-done.1
  569.8 0.0 slice-done.3
  569.8 0.0 copy-done.3
  569.9 0.0 copy-start.2
  569.9 5.6 fusion.5
  575.4 0.0 copy-done.2
  575.4 19.0 %fusion.3 = (f32[1536,8,128]{2,1,0:T(8,128)}, f32[1536,8,128]{2,1,0:T(8,128)}, f32[1536,8,128]{2,1,0:T(8,128)}, f32[1536,8,128]{2,1,0:T(8,128)}) fusion(bf16[1536,8,128]{2,1,0:T(8,128)(2,1)S(1)} %copy-done.2, f32[1536,8,128]{2,1,0:T(8,128)} %bitcast.119, f32[1536,8,128]{2,1,0:T(8,128)} %bitcast.115, bf16[1536,8,128]{2,1,0:T(8,128)(2,1)} %get-tuple-element.19, ...), kind=kLoop, calls=%fused_computation.9 | loop fusion | flops 25165824 | bytes 56623104 | tf_op jit(solution)/shard_map/add | solution.py:20
  594.4 0.0 all-gather.5.cloned.1.call-done.x
  594.4 0.0 copy-start
  594.4 4.6 copy-done
  599.0 5.5 shard_map.190.rest_0_
  604.5 54.7 %all-gather.3.cloned.1.call-done.x = bf16[6144,8,128]{2,1,0:T(8,128)(2,1)} async-done(((bf16[768,8,128]{2,1,0:T(8,128)(2,1)}), bf16[6144,8,128]{2,1,0:T(8,128)(2,1)}) %all-gather.3.cloned.1.call-update) | async-done | bytes 12582928 | tf_op jit(solution)/shard_map/all_gather | solution.py:333
  659.1 0.0 copy-start.1
  659.1 4.6 copy-done.1
  663.7 5.5 shard_map.191
  (2 shorter events, 0.0 us)
Async XLA Ops:
  7.2 587.2 %all-gather.5.cloned.1.call-start = ((), (), s32[]{:S(2)}) async-start(), calls=%async_computation.1 | async-start | bytes 14155776 | tf_op jit(solution)/shard_map/all_gather | solution.py:333
  529.1 130.0 %all-gather.3.cloned.1.call-start = ((), (), s32[]{:S(2)}) async-start(), calls=%async_computation | async-start | bytes 14155776 | tf_op jit(solution)/shard_map/all_gather | solution.py:333
  530.0 39.9 %slice-start = ((s8[6291456]{0:T(1024)(128)(4,1)}), s8[4194304]{0:T(1024)(128)(4,1)S(1)}, s32[]{:S(2)}) async-start(s8[6291456]{0:T(1024)(128)(4,1)} %bitcast.107), calls=%async_computation.2 | async-start | bytes 8388608
  530.0 39.8 %slice-start.2 = ((s8[6291456]{0:T(1024)(128)(4,1)}), s8[4194304]{0:T(1024)(128)(4,1)S(1)}, s32[]{:S(2)}) async-start(s8[6291456]{0:T(1024)(128)(4,1)} %bitcast.111), calls=%async_computation.4 | async-start | bytes 8388608
  550.0 19.8 %slice-start.1 = ((s8[6291456]{0:T(1024)(128)(4,1)}), s8[2097152]{0:T(1024)(128)(4,1)S(1)}, s32[]{:S(2)}) async-start(s8[6291456]{0:T(1024)(128)(4,1)} %bitcast.107), calls=%async_computation.3 | async-start | bytes 4194304
  550.0 19.8 %slice-start.3 = ((s8[6291456]{0:T(1024)(128)(4,1)}), s8[2097152]{0:T(1024)(128)(4,1)S(1)}, s32[]{:S(2)}) async-start(s8[6291456]{0:T(1024)(128)(4,1)} %bitcast.111), calls=%async_computation.5 | async-start | bytes 4194304
  550.0 19.8 %copy-start.3 = (bf16[1536,8,128]{2,1,0:T(8,128)(2,1)S(1)}, bf16[1536,8,128]{2,1,0:T(8,128)(2,1)}, u32[]{:S(2)}) copy-start(bf16[1536,8,128]{2,1,0:T(8,128)(2,1)} %get-tuple-element.20) | copy-start | bytes 9437188
  569.9 5.6 copy-start.2
  594.4 4.6 copy-start
  659.1 4.6 copy-start.1
Sparse Core Ops, SparseCore 0:
  529.3 64.5 all-gather.4
  595.5 63.6 all-gather.2

commit v2 on v1

--- a/solution.py
+++ b/solution.py
@@ -7,10 +7,10 @@
 from jax.experimental.pallas import tpu as pltpu
 from jax.sharding import PartitionSpec as P
 
+
 MESH = pl.DeviceIdType.MESH
 F32, BF16 = jnp.float32, jnp.bfloat16
 SPLIT = 2
-GATHERED = 2
 BATCH = 8
 SLOTS = 5
 
@@ -38,7 +38,8 @@
     weights = 3
     g, w, m, v = (refs[i * weights : (i + 1) * weights] for i in range(4))
     refs = refs[4 * weights :]
-    gathered, block_out, sums = refs[:GATHERED], refs[GATHERED:weights], refs[weights : 2 * weights]
+    landed, go_right, go_left, sums = (refs[i * weights : (i + 1) * weights] for i in range(4))
+    refs = refs[2 * weights :]
     (own, sib, s1, s2p, s2m, r1, r2p, r2m, mb, vb, wb, gb, new) = refs[2 * weights : 2 * weights + 13]
     (own_sem, sib_send, sib_recv, ring_send, ring_recv, mvw_sem, g_sem, ag_send, ag_recv, out_sem) = refs[2 * weights + 13 :]
 
@@ -47,14 +48,12 @@
     x, c = me // 2, me % 2
     right, left = (me + 2) % n, (me + n - 2) % n
     other = 2 * x + 1 - c
-    opposite = (me + n // 2) % n
     block = g[0].shape[0] // layers // n
     layer = block * n
     size = block // SPLIT
     half = size // 2
     per_weight = layers * SPLIT
     chunks = weights * per_weight
-    ag_chunks = GATHERED * per_weight
 
     barrier = pltpu.get_barrier_semaphore()
     for peer in (right, left, other):
@@ -178,48 +177,48 @@
     def sum_out(t, k):
         return pltpu.make_async_copy(gb.at[t % 2], sums[place(k)[0]].at[at_block(k)], g_sem.at[t % 2])
 
-    def block_copy(k):
+    def local_copy(k):
+        return pltpu.make_async_copy(new.at[k], landed[place(k)[0]].at[at_whole(k, me)], out_sem.at[k])
+
+    def compact(k):
+        _, at, s = place(k)
+        return pl.ds(at * (block // 2) + s * half, half)
+
+    def to_peer(k, i, src, dst, peer):
+        return remote(src, dst, ag_send.at[k, i], ag_recv.at[k, i], peer)
+
+    def spread(k, some=(0, 1, 2, 3, 4)):
+        which, ds = place(k)[0], at_whole(k, me)
+        front, back = landed[which].at[first(ds)], landed[which].at[last(ds)]
+        plan = (
+            (new.at[k, A], go_right[which].at[compact(k)], right),
+            (new.at[k, B], go_left[which].at[compact(k)], left),
+            (new.at[k, B], back, right),
+            (new.at[k, A], front, left),
+            (new.at[k], landed[which].at[ds], other),
+        )
+        return [to_peer(k, i, *plan[i]) for i in some]
+
+    def across(k):
         which = place(k)[0]
-        return pltpu.make_async_copy(new.at[k], block_out[which - GATHERED].at[at_block(k)], out_sem.at[k])
-
-    def local_copy(k):
-        return pltpu.make_async_copy(new.at[k], gathered[place(k)[0]].at[at_whole(k, me)], out_sem.at[k])
-
-    def spread(k, some=(0, 1, 2)):
-        to = gathered[place(k)[0]].at[at_whole(k, me)]
-        peers = right, left, other
-        return [remote(new.at[k], to, ag_send.at[k, i], ag_recv.at[k, i], peers[i]) for i in some]
-
-    def passed(k, i, owner, peer, part=None):
-        ds = at_whole(k, owner)
-        ref = gathered[place(k)[0]].at[part(ds) if part else ds]
-        return remote(ref, ref, ag_send.at[k, i], ag_recv.at[k, i], peer)
-
-    def forward(k):
-        return [passed(k, 3, left, right, first), passed(k, 4, right, left, last)]
-
-    def across(k):
-        return [passed(k, 5, left, other), passed(k, 6, right, other)]
-
-    def across_opposite(k):
-        return [passed(k, 7, opposite, other)]
-
-    ticks = range(-1, max(chunks + 3, ag_chunks + 8))
+        from_left, from_right = at_whole(k, left), at_whole(k, right)
+        at = landed[which].at
+        return [
+            to_peer(k, 5, go_right[which].at[compact(k)], at[first(from_left)], other),
+            to_peer(k, 6, go_left[which].at[compact(k)], at[last(from_right)], other),
+            to_peer(k, 7, at[last(from_left)], at[last(from_left)], other),
+            to_peer(k, 8, at[first(from_right)], at[first(from_right)], other),
+        ]
+
     load(-1)
-    for t in ticks:
+    for t in range(-1, chunks + 6):
         for copy in rings(t - 1):
             copy.wait()
         k = t - 6
-        if 0 <= k < ag_chunks:
-            for copy in spread(k, (0, 1)):
+        if 0 <= k < chunks:
+            for copy in spread(k, (0, 1, 2, 3)):
                 copy.wait_recv()
-            for copy in forward(k) + across(k):
-                copy.start()
-        k = t - 8
-        if 0 <= k < ag_chunks:
-            for copy in forward(k):
-                copy.wait_recv()
-            for copy in across_opposite(k):
+            for copy in across(k):
                 copy.start()
         load(t + 1)
         for k, js in work(t):
@@ -236,24 +235,19 @@
                 if k >= 2:
                     sum_out(t - 2, k - 2).wait()
                 stage3(t, k)
+                for copy in spread(k):
+                    copy.start()
                 sum_out(t, k).start()
-                if k < ag_chunks:
-                    for copy in spread(k):
-                        copy.start()
-                    local_copy(k).start()
-                else:
-                    block_copy(k).start()
+                local_copy(k).start()
 
     for k in range(max(chunks - 2, 0), chunks):
         sum_out(k + 3, k).wait()
-    for k in range(ag_chunks, chunks):
-        block_copy(k).wait()
-    for k in range(ag_chunks):
+    for k in range(chunks):
         local_copy(k).wait()
-        for copy in spread(k) + forward(k):
+        for copy in spread(k):
             copy.wait_send()
-        spread(k, (2,))[0].wait_recv()
-        for copy in across(k) + across_opposite(k):
+        spread(k, (4,))[0].wait_recv()
+        for copy in across(k):
             copy.wait()
 
 
@@ -263,17 +257,17 @@
     size = block // SPLIT
     count = len(weights)
     chunks = count * layers * SPLIT
-    ag_chunks = GATHERED * layers * SPLIT
     tile = (8, 128)
     buffer = lambda *lead, dtype=BF16: pltpu.VMEM((*lead, *tile), dtype)
+    array = lambda rows: jax.ShapeDtypeStruct((rows, *tile), BF16)
     dma = pltpu.SemaphoreType.DMA
     out = pl.pallas_call(
         functools.partial(kernel, n, layers),
-        out_shape=[jax.ShapeDtypeStruct(x.shape, BF16) for x in weights[:GATHERED]]
-        + [jax.ShapeDtypeStruct(x.shape, BF16) for x in m[GATHERED:]]
-        + [jax.ShapeDtypeStruct(x.shape, BF16) for x in m],
+        out_shape=[array(x.shape[0]) for x in weights]
+        + [array(x.shape[0] // 2) for x in m * 2]
+        + [array(x.shape[0]) for x in m],
         in_specs=[everywhere] * (4 * count),
-        out_specs=[everywhere] * (2 * count),
+        out_specs=[everywhere] * (4 * count),
         scratch_shapes=[
             buffer(2, 4, size),
             buffer(4, 4, size),
@@ -290,57 +284,112 @@
             dma((SLOTS, 4)),
             dma((2, 3)),
             dma((2,)),
-            dma((ag_chunks, 8)),
-            dma((ag_chunks, 8)),
+            dma((chunks, 9)),
+            dma((chunks, 9)),
             dma((chunks,)),
         ],
         compiler_params=pltpu.CompilerParams(collective_id=0, has_side_effects=True, vmem_limit_bytes=62 * 2**20),
     )(*terms, *weights, *m, *v)
-    return out[:GATHERED], out[GATHERED:count], out[count:]
-
-
-def copy_kernel(x, *rest):
-    rest[-1][...] = x[...]
-
-
-def copied(x, whole=None, part=0, parts=1, into=None):
-    steps = 8
-    size = x.shape[0] // steps
-    out = jax.ShapeDtypeStruct((x.shape[0] * parts, *x.shape[1:]), x.dtype)
-    extra = [] if into is None else [into]
+    return (out[i * count : (i + 1) * count] for i in range(4))
+
+
+def put(items, buffer, sems, out):
+    into, outof, at = [], [], 0
+    for i, (src, to) in enumerate(items):
+        via = buffer.at[pl.ds(at, src.shape[0])]
+        into.append(pltpu.make_async_copy(src, via, sems.at[0, i]))
+        outof.append(pltpu.make_async_copy(via, out.at[pl.ds(to, src.shape[0])], sems.at[1, i]))
+        at += src.shape[0]
+    for copy in into:
+        copy.start()
+    for arrival, copy in zip(into, outof, strict=True):
+        arrival.wait()
+        copy.start()
+    for copy in outof:
+        copy.wait()
+
+
+def near_kernel(n, layers, landed, go_right, go_left, out, buffer, sems):
+    me = lax.axis_index("dp")
+    other = me + 1 - 2 * (me % 2)
+    block = landed.shape[0] // layers // n
+    half = block // SPLIT // 2
+    items = []
+    for layer in range(layers):
+        base = layer * n * block
+        for owner in (me, other, (other + 2) % n, (other + n - 2) % n):
+            at = base + owner * block
+            items.append((landed.at[pl.ds(at, block)], at))
+        for s in range(SPLIT):
+            right, left = (base + owner % n * block + 2 * s * half for owner in (me + 2, me + n - 2))
+            compact = pl.ds((layer * SPLIT + s) * half, half)
+            items += [
+                (landed.at[pl.ds(right, half)], right),
+                (go_left.at[compact], right + half),
+                (go_right.at[compact], left),
+                (landed.at[pl.ds(left + half, half)], left + half),
+            ]
+    put(items, buffer, sems, out)
+
+
+def far_kernel(n, layers, front, back, other_front, other_back, _, out, buffer, sems):
+    me = lax.axis_index("dp")
+    other = me + 1 - 2 * (me % 2)
+    block = out.shape[0] // layers // n
+    half = block // SPLIT // 2
+    items = []
+    for layer in range(layers):
+        for s in range(SPLIT):
+            compact = pl.ds((layer * SPLIT + s) * half, half)
+            for owner, x, y in ((me, front, back), (other, other_front, other_back)):
+                at = (layer * n + (owner + n // 2) % n) * block + 2 * s * half
+                items += [(x.at[compact], at), (y.at[compact], at + half)]
+    put(items, buffer, sems, out)
+
+
+def placed(body, n, layers, count, share, like, operands, into=None):
+    everywhere = pl.BlockSpec(memory_space=pl.ANY)
+    operands = [*operands, *([] if into is None else [into])]
     return pl.pallas_call(
-        copy_kernel,
-        grid=(steps,),
-        out_shape=out,
-        in_specs=[pl.BlockSpec((size, 8, 128), lambda i: (i, 0, 0))] + [pl.BlockSpec(memory_space=pl.ANY)] * len(extra),
-        out_specs=pl.BlockSpec((size, 8, 128), lambda i: (i + part * steps, 0, 0)),
-        input_output_aliases={1: 0} if extra else {},
-        cost_estimate=pl.CostEstimate(flops=0, bytes_accessed=2 * x.size * x.dtype.itemsize, transcendentals=0),
-        compiler_params=pltpu.CompilerParams(vmem_limit_bytes=32 * 2**20),
-    )(x, *extra)
+        functools.partial(body, n, layers),
+        out_shape=jax.ShapeDtypeStruct(like.shape, like.dtype),
+        in_specs=[everywhere] * len(operands),
+        out_specs=everywhere,
+        scratch_shapes=[pltpu.VMEM((int(share * like.shape[0]), 8, 128), BF16), pltpu.SemaphoreType.DMA((2, count))],
+        input_output_aliases={} if into is None else {len(operands) - 1: 0},
+        cost_estimate=pl.CostEstimate(flops=0, bytes_accessed=int(2 * share * like.size * like.dtype.itemsize), transcendentals=0),
+        compiler_params=pltpu.CompilerParams(vmem_limit_bytes=67043328),
+    )(*operands)
 
 
 def solution(mesh):
     n = mesh.shape["dp"]
+    to_right = [(i, (i + 2) % n) for i in range(n)]
+    to_left = [(i, (i - 2) % n) for i in range(n)]
+    to_other = [(i, i ^ 1) for i in range(n)]
 
     def step(*arrays):
         terms, weights, m, v = (arrays[i : i + 3] for i in (0, 3, 6, 9))
         layers = weights[0].shape[0]
-        m_tiles, v_tiles = [tiles(a) for a in m], [tiles(a) for a in v]
-        landed, blocks, sums = exchange(n, layers, [tiles(t[0]) for t in terms], [tiles(a) for a in weights], m_tiles, v_tiles)
-        whole = []
-        for one in blocks:
-            parts = [lax.all_gather(p, "dp", axis=0, tiled=True) for p in jnp.split(one, layers)]
-            result = None
-            for i, part in enumerate(parts):
-                result = copied(part, part=i, parts=layers, into=result)
-            whole.append(result)
-        whole = [copied(a) for a in landed] + whole
+        m_tiles, v_tiles, w_tiles = ([tiles(a) for a in group] for group in (m, v, weights))
+        landed, go_right, go_left, sums = exchange(n, layers, [tiles(t[0]) for t in terms], w_tiles, m_tiles, v_tiles)
+        passed = []
+        for r, l in zip(go_right, go_left, strict=True):
+            front = lax.ppermute(r, "dp", to_right)
+            back = lax.ppermute(l, "dp", to_left)
+            passed.append((front, back))
         new_m, new_v = [], []
         for mm, vv, s in zip(m_tiles, v_tiles, sums, strict=True):
             _, a, b = adamw(jnp.zeros((), F32), mm, vv, s.astype(F32))
             new_m.append(a)
             new_v.append(b)
+        near = []
+        for like, *x in zip(w_tiles, landed, go_right, go_left, strict=True):
+            near.append(placed(near_kernel, n, layers, 4 * layers * (1 + SPLIT), 0.75, like, x))
+        whole = []
+        for like, out, pair in zip(w_tiles, near, passed, strict=True):
+            pair = [*pair, *(lax.ppermute(a, "dp", to_other) for a in pair)]
+            whole.append(placed(far_kernel, n, layers, 4 * layers * SPLIT, 0.25, like, pair, out))
         return (
             *(untiles(a, like.shape) for a, like in zip(whole, weights, strict=True)),
             *(untiles(a, like.shape) for a, like in zip(new_m, m, strict=True)),

time: 676 us -> 663 us (0.981)
  between operations: 14.2 us -> 0.76 us
  local copies, waits for them, and re-layouts: 12.9 us -> 0.01 us
  waiting for transfers between devices: 55.4 us -> 45 us
  starting transfers between devices: 0.13 us -> 10.4 us
  Pallas kernels: 569 us -> 578 us
    all_gather x2 -> x0, waiting for transfers between devices: 54.7 us -> none  [step(): lax.all_gather(p, 'dp', axis=0, tiled=True)]
    ppermute x0 -> x12, waiting for transfers between devices: none -> 45 us  [the longest x3 45 us: step(): front = lax.ppermute(r, 'dp', to_right)]
    ppermute x0 -> x12, starting transfers between devices: none -> 10.4 us  [the longest x3 5.37 us: step(): back = lax.ppermute(l, 'dp', to_left)]
    unnamed x16 -> x2, local copies, waits for them, and re-layouts: 9.18 us -> 0.01 us
    pallas_call x5 -> x7, Pallas kernels: 569 us -> 578 us  [the longest x1 521 us: exchange(): pl.pallas_call(functools.partial(kernel, n, layers), out_shape=[array(x.s...]
  transfers between devices with their start and end apart: 2 -> 12, of which waited for: 1 -> 2; matrix products, arithmetic and copies ran while one was open for 4% -> 4% of each run, Pallas kernels for 7% -> 8%
where the time goes in v2:
time: 663 us
  Pallas kernels  578 us (87%)
  waiting for transfers between devices  45 us (7%)
  other arithmetic  29.1 us (4%)
  starting transfers between devices  10.4 us (2%)
    pallas_call x1, Pallas kernels, exchange(): pl.pallas_call(functools.partial(kernel, n, layers), out_shape=[array(x.s...  521 us
    pallas_call x6, Pallas kernels, placed(): pl.pallas_call(functools.partial(body, n, layers), out_shape=jax.ShapeDty...  57.2 us
    ppermute x3, waiting for transfers between devices, step(): front = lax.ppermute(r, 'dp', to_right)  45 us
    add x2, other arithmetic, adamw(): v = 0.95 * v + 0.05 * g * g  29.1 us
  transfers between devices with their start and end apart: 12, of which 2 were waited for; matrix products, arithmetic and copies ran while one was open for 4% of the time, Pallas kernels for 8%

profile of v2, /device:TPU:113, one launch (start us, length us, event | category | flops | bytes accessed | tf_op | source)
XLA Modules:
  0.0 663.2 jit_solution(11253186649528948181)
XLA Ops:
  0.6 520.7 %shard_map.187 = (bf16[12288,8,128]{2,1,0:T(8,128)(2,1)}, bf16[12288,8,128]{2,1,0:T(8,128)(2,1)}, bf16[12288,8,128]{2,1,0:T(8,128)(2,1)}, bf16[768,8,128]{2,1,0:...) custom-call(bf16[12288,8,128]{2,1,0:T(8,128)(2,1)} %bitcast.120, ...), custom_call_target="tpu_custom_call" | custom-call | tf_op jit(solution)/shard_map/pallas_call | solution.py:264
  521.3 1.1 collective-permute-start.8
  522.5 1.6 collective-permute-start.9
  524.1 0.0 collective-permute-start.4
  524.1 2.7 collective-permute-start.5
  526.8 0.0 collective-permute-start
  526.8 32.0 %collective-permute-done.8.front = bf16[768,8,128]{2,1,0:T(8,128)(2,1)} collective-permute-done((bf16[768,8,128]{2,1,0:T(8,128)(2,1)}, bf16[768,8,128]{2,1,0:T(8,128)(2,1)}, u32[]{:S(2)}, u32[]{:S(2)}) %collective-permute-start.8) | collective-permute-done | bytes 1572896 | tf_op jit(solution)/shard_map/ppermute | solution.py:378
  558.7 1.1 collective-permute-start.1
  559.8 0.0 collective-permute-done.9.back
  559.8 1.9 collective-permute-start.10
  561.7 13.5 %shard_map.192._ = bf16[12288,8,128]{2,1,0:T(8,128)(2,1)} custom-call(bf16[12288,8,128]{2,1,0:T(8,128)(2,1)} %get-tuple-element.29.landed, bf16[768,8,128]{2,1,0:T(8,128)(2,1)} %get-tuple-element.27.go_right, bf16[768,8,128]{2,1,0:T(8,128)(2,1)} %get-tuple-element.28.go_left), custom_call_target="tpu_custom_call" | custom-call | bytes 37748736 | tf_op jit(solution)/shard_map/pallas_call | solution.py:353
  575.2 13.6 %shard_map.190._ = bf16[12288,8,128]{2,1,0:T(8,128)(2,1)} custom-call(bf16[12288,8,128]{2,1,0:T(8,128)(2,1)} %get-tuple-element.26.landed, bf16[768,8,128]{2,1,0:T(8,128)(2,1)} %get-tuple-element.24.go_right, bf16[768,8,128]{2,1,0:T(8,128)(2,1)} %get-tuple-element.25.go_left), custom_call_target="tpu_custom_call" | custom-call | bytes 37748736 | tf_op jit(solution)/shard_map/pallas_call | solution.py:353
  588.9 13.6 %shard_map.188._ = bf16[12288,8,128]{2,1,0:T(8,128)(2,1)} custom-call(bf16[12288,8,128]{2,1,0:T(8,128)(2,1)} %get-tuple-element.23.landed, bf16[768,8,128]{2,1,0:T(8,128)(2,1)} %get-tuple-element.21.go_right, bf16[768,8,128]{2,1,0:T(8,128)(2,1)} %get-tuple-element.22.go_left), custom_call_target="tpu_custom_call" | custom-call | bytes 37748736 | tf_op jit(solution)/shard_map/pallas_call | solution.py:353
  602.5 0.0 copy-start
  602.5 10.1 %fusion.5 = (f32[1536,8,128]{2,1,0:T(8,128)}, f32[1536,8,128]{2,1,0:T(8,128)}) fusion(bf16[1536,8,128]{2,1,0:T(8,128)(2,1)} %get-tuple-element.32, f32[1536,8,128]{2,1,0:T(8,128)} %bitcast.111, f32[1536,8,128]{2,1,0:T(8,128)} %bitcast.109), kind=kLoop, calls=%fused_computation.11 | loop fusion | flops 12582912 | bytes 28311552 | tf_op jit(solution)/shard_map/add | solution.py:20
  612.6 0.0 collective-permute-done.4.front
  612.6 0.1 collective-permute-start.11
  612.7 0.0 collective-permute-done.5.back
  612.7 0.5 collective-permute-start.6
  613.2 13.0 %collective-permute-done.front = bf16[768,8,128]{2,1,0:T(8,128)(2,1)} collective-permute-done((bf16[768,8,128]{2,1,0:T(8,128)(2,1)}, bf16[768,8,128]{2,1,0:T(8,128)(2,1)}, u32[]{:S(2)}, u32[]{:S(2)}) %collective-permute-start) | collective-permute-done | bytes 1572896 | tf_op jit(solution)/shard_map/ppermute | solution.py:378
  626.2 1.0 collective-permute-start.7
  627.2 0.0 collective-permute-done.1.back
  627.2 0.0 collective-permute-start.2
  627.2 0.0 collective-permute-done.10.other_front
  627.2 0.5 collective-permute-start.3
  627.7 0.0 copy-done
  627.7 19.0 %fusion.3 = (f32[1536,8,128]{2,1,0:T(8,128)}, f32[1536,8,128]{2,1,0:T(8,128)}, f32[1536,8,128]{2,1,0:T(8,128)}, f32[1536,8,128]{2,1,0:T(8,128)}) fusion(bf16[1536,8,128]{2,1,0:T(8,128)(2,1)S(1)} %copy-done, f32[1536,8,128]{2,1,0:T(8,128)} %bitcast.117, f32[1536,8,128]{2,1,0:T(8,128)} %bitcast.113, bf16[1536,8,128]{2,1,0:T(8,128)(2,1)} %get-tuple-element.31, ...), kind=kLoop, calls=%fused_computation.9 | loop fusion | flops 25165824 | bytes 56623104 | tf_op jit(solution)/shard_map/add | solution.py:20
  646.6 0.0 collective-permute-done.11.other_back
  646.6 5.5 shard_map.193
  652.1 0.0 collective-permute-done.6.other_front
  652.2 0.0 collective-permute-done.7.other_back
  652.2 5.5 shard_map.191
  657.7 0.0 collective-permute-done.2.other_front
  657.7 0.0 collective-permute-done.3.other_back
  657.7 5.5 shard_map.189
Async XLA Ops:
  521.3 37.4 %collective-permute-start.8 = (bf16[768,8,128]{2,1,0:T(8,128)(2,1)}, bf16[768,8,128]{2,1,0:T(8,128)(2,1)}, u32[]{:S(2)}, u32[]{:S(2)}) collective-permute-start(bf16[768,8,128]{2,1,0:T(8,128)(2,1)} %get-tuple-element.27.go_right), channel_id=1, source_target_pairs={{0,2},{1,3},{2,4},{3,5},{4,6},{5,7},{6,0},{7,1},{8,10},{9,11},{10,... | collective-permute-start | bytes 4718600 | tf_op jit(solution)/shard_map/ppermute | solution.py:378
  522.5 37.4 %collective-permute-start.9 = (bf16[768,8,128]{2,1,0:T(8,128)(2,1)}, bf16[768,8,128]{2,1,0:T(8,128)(2,1)}, u32[]{:S(2)}, u32[]{:S(2)}) collective-permute-start(bf16[768,8,128]{2,1,0:T(8,128)(2,1)} %get-tuple-element.28.go_left), channel_id=1, source_target_pairs={{0,6},{1,7},{2,0},{3,1},{4,2},{5,3},{6,4},{7,5},{8,14},{9,15},{10,... | collective-permute-start | bytes 4718600 | tf_op jit(solution)/shard_map/ppermute | solution.py:379
  524.1 88.5 %collective-permute-start.4 = (bf16[768,8,128]{2,1,0:T(8,128)(2,1)}, bf16[768,8,128]{2,1,0:T(8,128)(2,1)}, u32[]{:S(2)}, u32[]{:S(2)}) collective-permute-start(bf16[768,8,128]{2,1,0:T(8,128)(2,1)} %get-tuple-element.24.go_right), channel_id=1, source_target_pairs={{0,2},{1,3},{2,4},{3,5},{4,6},{5,7},{6,0},{7,1},{8,10},{9,11},{10,... | collective-permute-start | bytes 4718600 | tf_op jit(solution)/shard_map/ppermute | solution.py:378
  524.1 88.6 %collective-permute-start.5 = (bf16[768,8,128]{2,1,0:T(8,128)(2,1)}, bf16[768,8,128]{2,1,0:T(8,128)(2,1)}, u32[]{:S(2)}, u32[]{:S(2)}) collective-permute-start(bf16[768,8,128]{2,1,0:T(8,128)(2,1)} %get-tuple-element.25.go_left), channel_id=1, source_target_pairs={{0,6},{1,7},{2,0},{3,1},{4,2},{5,3},{6,4},{7,5},{8,14},{9,15},{10,... | collective-permute-start | bytes 4718600 | tf_op jit(solution)/shard_map/ppermute | solution.py:379
  526.8 99.4 %collective-permute-start = (bf16[768,8,128]{2,1,0:T(8,128)(2,1)}, bf16[768,8,128]{2,1,0:T(8,128)(2,1)}, u32[]{:S(2)}, u32[]{:S(2)}) collective-permute-start(bf16[768,8,128]{2,1,0:T(8,128)(2,1)} %get-tuple-element.21.go_right), channel_id=1, source_target_pairs={{0,2},{1,3},{2,4},{3,5},{4,6},{5,7},{6,0},{7,1},{8,10},{9,11},{10,... | collective-permute-start | bytes 4718600 | tf_op jit(solution)/shard_map/ppermute | solution.py:378
  558.7 68.4 %collective-permute-start.1 = (bf16[768,8,128]{2,1,0:T(8,128)(2,1)}, bf16[768,8,128]{2,1,0:T(8,128)(2,1)}, u32[]{:S(2)}, u32[]{:S(2)}) collective-permute-start(bf16[768,8,128]{2,1,0:T(8,128)(2,1)} %get-tuple-element.22.go_left), channel_id=1, source_target_pairs={{0,6},{1,7},{2,0},{3,1},{4,2},{5,3},{6,4},{7,5},{8,14},{9,15},{10,... | collective-permute-start | bytes 4718600 | tf_op jit(solution)/shard_map/ppermute | solution.py:379
  559.8 67.3 %collective-permute-start.10 = (bf16[768,8,128]{2,1,0:T(8,128)(2,1)}, bf16[768,8,128]{2,1,0:T(8,128)(2,1)}, u32[]{:S(2)}, u32[]{:S(2)}) collective-permute-start(bf16[768,8,128]{2,1,0:T(8,128)(2,1)} %collective-permute-done.8.front), channel_id=1, source_target_pairs={{0,1},{1,0},{2,3},{3,2},{4,5},{5,4},{6,7},{7,6},{8,9},{9,8},{10,11... | collective-permute-start | bytes 4718600 | tf_op jit(solution)/shard_map/ppermute | solution.py:391
  602.5 25.2 %copy-start = (bf16[1536,8,128]{2,1,0:T(8,128)(2,1)S(1)}, bf16[1536,8,128]{2,1,0:T(8,128)(2,1)}, u32[]{:S(2)}) copy-start(bf16[1536,8,128]{2,1,0:T(8,128)(2,1)} %get-tuple-element.30) | copy-start | bytes 9437188
  612.6 34.0 %collective-permute-start.11 = (bf16[768,8,128]{2,1,0:T(8,128)(2,1)}, bf16[768,8,128]{2,1,0:T(8,128)(2,1)}, u32[]{:S(2)}, u32[]{:S(2)}) collective-permute-start(bf16[768,8,128]{2,1,0:T(8,128)(2,1)} %collective-permute-done.9.back), channel_id=1, source_target_pairs={{0,1},{1,0},{2,3},{3,2},{4,5},{5,4},{6,7},{7,6},{8,9},{9,8},{10,11... | collective-permute-start | bytes 4718600 | tf_op jit(solution)/shard_map/ppermute | solution.py:391
  612.7 39.4 %collective-permute-start.6 = (bf16[768,8,128]{2,1,0:T(8,128)(2,1)}, bf16[768,8,128]{2,1,0:T(8,128)(2,1)}, u32[]{:S(2)}, u32[]{:S(2)}) collective-permute-start(bf16[768,8,128]{2,1,0:T(8,128)(2,1)} %collective-permute-done.4.front), channel_id=1, source_target_pairs={{0,1},{1,0},{2,3},{3,2},{4,5},{5,4},{6,7},{7,6},{8,9},{9,8},{10,11... | collective-permute-start | bytes 4718600 | tf_op jit(solution)/shard_map/ppermute | solution.py:391
  626.2 26.0 %collective-permute-start.7 = (bf16[768,8,128]{2,1,0:T(8,128)(2,1)}, bf16[768,8,128]{2,1,0:T(8,128)(2,1)}, u32[]{:S(2)}, u32[]{:S(2)}) collective-permute-start(bf16[768,8,128]{2,1,0:T(8,128)(2,1)} %collective-permute-done.5.back), channel_id=1, source_target_pairs={{0,1},{1,0},{2,3},{3,2},{4,5},{5,4},{6,7},{7,6},{8,9},{9,8},{10,11... | collective-permute-start | bytes 4718600 | tf_op jit(solution)/shard_map/ppermute | solution.py:391
  627.2 30.5 %collective-permute-start.2 = (bf16[768,8,128]{2,1,0:T(8,128)(2,1)}, bf16[768,8,128]{2,1,0:T(8,128)(2,1)}, u32[]{:S(2)}, u32[]{:S(2)}) collective-permute-start(bf16[768,8,128]{2,1,0:T(8,128)(2,1)} %collective-permute-done.front), channel_id=1, source_target_pairs={{0,1},{1,0},{2,3},{3,2},{4,5},{5,4},{6,7},{7,6},{8,9},{9,8},{10,11... | collective-permute-start | bytes 4718600 | tf_op jit(solution)/shard_map/ppermute | solution.py:391
  627.2 30.5 %collective-permute-start.3 = (bf16[768,8,128]{2,1,0:T(8,128)(2,1)}, bf16[768,8,128]{2,1,0:T(8,128)(2,1)}, u32[]{:S(2)}, u32[]{:S(2)}) collective-permute-start(bf16[768,8,128]{2,1,0:T(8,128)(2,1)} %collective-permute-done.1.back), channel_id=1, source_target_pairs={{0,1},{1,0},{2,3},{3,2},{4,5},{5,4},{6,7},{7,6},{8,9},{9,8},{10,11... | collective-permute-start | bytes 4718600 | tf_op jit(solution)/shard_map/ppermute | solution.py:391
